TPU v7x, 32 devices: a whole 2x2x4 slice. The times are simulated.
32 devices in a mesh: arow: 4 (over z), acol: 8 (over y, x, core).
Axes of the slice: x: 2, y: 2, z: 4, core: 2. Of those that a mesh axis runs over, the one named last changes fastest.
Arguments:
- row_data: bfloat16 [65536, 128], P(('arow', 'acol')), may hold values from -96 to 96
- row_baseline: int32 [65536], P(('arow', 'acol')), may hold values from 0 to 131071, as said below
- pair_table: int32 [131072, 2], P(('arow', 'acol')), may hold values from 0 to 2047, as said below
- lengths: int32 [131072], P(('arow', 'acol')), may hold values from 1 to 8
- model_vis: bfloat16 [2048, 2048, 128], P('arow', 'acol'), may hold values from -6 to 6
- gains: float32 [2048, 128], P(('arow', 'acol')), may hold values from -6 to 6
Outputs:
- new_gains: float32 [2048, 128], P(('arow', 'acol'))
Inputs may be any that keep to these rules, and one draw needn't show every extreme that they name: `pair_table`: slot j belongs to tile o = j // 4096; its first antenna lies in 512 * (o // 8) to 512 * (o // 8 + 1) - 1, its second in 256 * (o % 8) to 256 * (o % 8 + 1) - 1, and the two differ. `row_baseline`: the rows of one device name slots of one tile at most 256 times; one tile is named exactly 256 times by the rows of every device.
All inputs are finite; a program needn't handle non-finite values.
Results may differ from a plain program's by a relative error of at most 0.0003.
Values may be sent and summed in bfloat16 or wider, within the bound.
A program may use at most 128 MiB of HBM per device.

v0:
```python
import math

import jax
import jax.numpy as jnp
from jax import lax
from jax.sharding import PartitionSpec as P

RIDGE = 1.0


def local(row_data, row_baseline, pair_table, lengths, model_vis, gains):
    row_count = lax.axis_size("arow")
    col_count = lax.axis_size("acol")
    devices = row_count * col_count
    count_rows = row_data.shape[0]
    width = row_data.shape[1]
    half = width // 2
    slots = lengths.shape[0]
    capacity = 4 * count_rows // devices
    row_block = model_vis.shape[0]
    col_block = model_vis.shape[1]
    my_row = lax.axis_index("arow")
    my_col = lax.axis_index("acol")
    owner = row_baseline // slots
    local_id = row_baseline - owner * slots
    hits = (owner[:, None] == jnp.arange(devices, dtype=jnp.int32)[None, :]).astype(jnp.bfloat16)
    step_rows = math.gcd(count_rows, 128)
    block_count = count_rows // step_rows
    blocks = hits.reshape(block_count, step_rows, devices)
    positions = jnp.arange(step_rows, dtype=jnp.int32)
    lower = (positions[:, None] > positions[None, :]).astype(jnp.bfloat16)
    within = jnp.einsum("ij,bjd->bid", lower, blocks, preferred_element_type=jnp.float32)
    per_block = jnp.sum(blocks, axis=1, dtype=jnp.float32)
    before = jnp.cumsum(per_block, axis=0) - per_block
    ranking = jnp.sum((within + before[:, None, :]) * blocks.astype(jnp.float32), axis=2).reshape(
        count_rows
    )
    target = owner * capacity + ranking.astype(jnp.int32)
    code = local_id + 1
    codes = jnp.stack([code // 64, code % 64], axis=1).astype(jnp.bfloat16)
    groups = math.gcd(devices, 16)
    span = devices * capacity // groups

    def place(group):
        wanted = group * span + jnp.arange(span, dtype=jnp.int32)
        table = (target[None, :] == wanted[:, None]).astype(jnp.bfloat16)
        placed = jnp.dot(table, row_data, preferred_element_type=jnp.float32).astype(jnp.bfloat16)
        tagged = jnp.dot(table, codes, preferred_element_type=jnp.float32)
        return (placed, tagged)

    outgoing, tags = lax.map(place, jnp.arange(groups, dtype=jnp.int32))
    outgoing = outgoing.reshape(devices * capacity, width)
    labels = (tags[..., 0] * 64.0 + tags[..., 1]).astype(jnp.int32).reshape(devices * capacity) - 1
    arrived, names = (
        lax.all_to_all(
            outgoing.reshape(devices, capacity, width),
            ("arow", "acol"),
            split_axis=0,
            concat_axis=0,
            tiled=True,
        ),
        lax.all_to_all(
            labels.reshape(devices, capacity),
            ("arow", "acol"),
            split_axis=0,
            concat_axis=0,
            tiled=True,
        ),
    )
    arrived = arrived.reshape(devices * capacity, width)
    names = names.reshape(devices * capacity)
    valid = names >= 0
    safe = jnp.clip(names, 0, slots - 1)
    slot_info = jnp.concatenate([pair_table, lengths[:, None]], axis=1)
    found = jnp.take(slot_info, safe, axis=0)
    first = jnp.clip(found[:, 0] - my_row * row_block, 0, row_block - 1)
    second = jnp.clip(found[:, 1] - my_col * col_block, 0, col_block - 1)
    weight = jnp.where(valid, found[:, 2], 0).astype(jnp.float32)
    every = lax.all_gather(gains, ("arow", "acol"), axis=0, tiled=True)
    column_gains = lax.dynamic_slice_in_dim(every, my_col * col_block, col_block, 0)
    pick_col = (second[:, None] == jnp.arange(col_block, dtype=jnp.int32)[None, :]).astype(
        jnp.float32
    )
    row_gain = jnp.dot(
        pick_col, column_gains, precision=lax.Precision.HIGHEST, preferred_element_type=jnp.float32
    )
    model_rows = jnp.take(
        model_vis.reshape(row_block * col_block, width), first * col_block + second, axis=0
    )
    m_re = model_rows[:, :half].astype(jnp.float32)
    m_im = model_rows[:, half:].astype(jnp.float32)
    g_re = row_gain[:, :half]
    g_im = row_gain[:, half:]
    c_re = m_re * g_re + m_im * g_im
    c_im = m_re * g_im - m_im * g_re
    r_re = arrived[:, :half].astype(jnp.float32) * weight[:, None]
    r_im = arrived[:, half:].astype(jnp.float32) * weight[:, None]
    values = jnp.concatenate(
        [
            c_re * r_re - c_im * r_im,
            c_re * r_im + c_im * r_re,
            weight[:, None] * (c_re * c_re + c_im * c_im),
        ],
        axis=1,
    )
    pick_row = (first[None, :] == jnp.arange(row_block, dtype=jnp.int32)[:, None]).astype(
        jnp.float32
    )
    totals = jnp.dot(
        pick_row, values, precision=lax.Precision.HIGHEST, preferred_element_type=jnp.float32
    )
    numer = totals[:, :width]
    denom = totals[:, width:]
    numer, denom = lax.psum((numer, denom), "acol")
    share = row_block // col_count
    numer = lax.dynamic_slice_in_dim(numer, my_col * share, share, 0)
    denom = lax.dynamic_slice_in_dim(denom, my_col * share, share, 0)
    return jnp.concatenate(
        [numer[:, :half] / (denom + RIDGE), numer[:, half:] / (denom + RIDGE)], axis=1
    )


def solution(mesh):
    placed = (
        P(("arow", "acol"), None),
        P(("arow", "acol")),
        P(("arow", "acol"), None),
        P(("arow", "acol")),
        P("arow", "acol", None),
        P(("arow", "acol"), None),
    )
    return jax.shard_map(
        local, mesh=mesh, in_specs=placed, out_specs=P(("arow", "acol"), None), check_vma=False
    )
```

profile of v0, /device:TPU:0, one launch (start us, length us, event | category | flops | bytes accessed | tf_op | source)
XLA Modules:
  0.0 531.5 jit_solution(483655217040452650)
XLA Ops:
  6.5 0.7 fusion.50
  7.7 0.7 bitcast_add_fusion
  8.5 71.8 %while.12 = (s32[]{:T(128)}, bf16[16,512,128]{2,1,0:T(8,128)(2,1)}, f32[16,512,2]{1,2,0:T(2,128)S(1)}, s32[2048]{0:T(1024)S(1)}, s32[16]{0:T(128)S(1)}, /*index=...) while((s32[]{:T(128)}, bf16[16,512,128]{2,1,0:T(8,128)(2,1)}, ...), condition=%wide.region_4.5_spmd, body=%wide.region_3.4_spmd.sunk | while | flops 274792960 | bytes 690813 | solution.py:51
  9.7 2.4 fusion.73
  12.2 0.8 fusion.74
  14.2 2.5 fusion.73
  16.7 0.8 fusion.74
  18.7 2.5 fusion.73
  21.1 0.8 fusion.74
  23.2 2.5 fusion.73
  25.6 0.8 fusion.74
  27.7 2.5 fusion.73
  30.1 0.8 fusion.74
  32.2 2.4 fusion.73
  34.6 0.8 fusion.74
  36.6 2.5 fusion.73
  39.1 0.8 fusion.74
  41.1 2.5 fusion.73
  43.6 0.8 fusion.74
  45.6 2.5 fusion.73
  48.1 0.8 fusion.74
  50.1 2.5 fusion.73
  52.6 0.8 fusion.74
  54.6 2.5 fusion.73
  57.0 0.8 fusion.74
  59.1 2.5 fusion.73
  61.5 0.8 fusion.74
  63.6 2.5 fusion.73
  66.0 0.8 fusion.74
  68.0 2.5 fusion.73
  70.5 0.8 fusion.74
  72.5 2.5 fusion.73
  75.0 0.8 fusion.74
  77.0 2.5 fusion.73
  79.5 0.8 fusion.74
  80.3 0.7 convert_add_fusion
  81.0 7.3 %all-to-all-start = ((s32[32,1,256]{2,1,0:T(1,128)}), s32[32,1,256]{2,1,0:T(1,128)S(1)}, u32[]{:S(2)}, u32[]{:S(2)}) async-start(s32[32,1,256]{2,1,0:T(1,128)} %bitcast.7), calls=%async_computation | async-start | bytes 65536 | tf_op jit(solution)/shard_map/all_to_all | solution.py:62
  88.3 0.7 all-gather.2.cloned.1.call-update
  89.1 0.6 copy.31
  89.7 4.1 copy.33
  93.8 1.7 all-to-all-done
  95.5 4.3 all-to-all-start.1
  100.1 2.6 copy.28
  102.7 3.3 fusion.31
  106.1 1.7 copy.35
  107.9 27.7 %gather_fusion = s32[8192,3]{1,0:T(8,128)} fusion(s32[4096,3]{1,0:T(8,128)S(1)} %copy.31, s32[8192]{0:T(1024)S(1)} %broadcast_clamp_fusion.1), kind=kCustom, calls=%fused_computation | custom fusion | bytes 229376 | tf_op jit(solution)/shard_map/jit(_take)/gather | solution.py:75
  135.6 6.2 %broadcast_select_fusion = s32[8192,3]{1,0:T(8,128)S(1)} fusion(s32[8192,3]{1,0:T(8,128)} %gather_fusion, pred[8192]{0:T(1024)(128)(4,1)S(1)} %compare_and_fusion), kind=kLoop, calls=%fused_computation.51 | loop fusion | flops 24576 | bytes 204800 | tf_op jit(solution)/shard_map/jit(_take)/select_n | solution.py:75
  141.8 2.2 fusion.33
  144.1 4.9 fusion.58
  149.0 3.2 and_reduce_fusion
  152.2 284.9 %gather_fusion.1 = bf16[8192,128]{1,0:T(8,128)(2,1)S(1)} fusion(bf16[131072,128]{1,0:T(8,128)(2,1)} %bitcast.45, s32[8192]{0:T(1024)S(1)} %broadcast_clamp_fusion), kind=kCustom, calls=%fused_computation.1 | custom fusion | bytes 4227072 | tf_op jit(solution)/shard_map/jit(_take)/gather | solution.py:87
  437.1 3.0 copy.32
  440.0 1.8 broadcast_select_fusion.1
  441.9 7.3 %fusion.25 = f32[8192,128]{0,1:T(8,128)} fusion(s32[8192]{0:T(1024)S(1)} %get-tuple-element.47, f32[2048,128]{1,0:T(8,128)} %all-gather.2.cloned.1.call-done, s32[]{:T(128)S(6)} %select_n.65), kind=kOutput, calls=%fused_computation.22 | convolution fusion | flops 3223322624 | bytes 4358148 | tf_op jit(solution)/shard_map/dot_general | solution.py:84
  449.2 1.9 copy.37
  451.2 0.9 copy-done
  452.0 1.1 multiply_subtract_fusion
  453.1 0.8 multiply_add_fusion
  453.9 9.6 %fusion.23 = f32[512,192]{0,1:T(8,128)S(1)} fusion(s32[8192]{0:T(1024)S(1)} %get-tuple-element.46, f32[8192,64]{0,1:T(8,128)S(1)} %get-tuple-element.68, f32[8192,64]{0,1:T(8,128)S(1)} %get-tuple-element.67, f32[8192,64]{0,1:T(8,128)S(1)} %get-tuple-element.64), kind=kOutput, calls=%fused_computation.17 | convolution fusion | flops 9671016448 | bytes 6717440 | tf_op jit(solution)/shard_map/dot_general | solution.py:109
  463.5 0.7 slice.73
  464.2 0.6 slice.74
  464.9 58.1 %all-reduce.3.cloned.1.call-done = (f32[512,128]{0,1:T(8,128)}, f32[512,64]{0,1:T(8,128)}) async-done(((f32[512,128]{0,1:T(8,128)}, f32[512,64]{0,1:T(8,128)}), (f32[512,128]{0,1:T(8,128)}, f32[512,64]{0,1:T(8,128)})) %all-reduce.3.cloned.1.call-update) | async-done | bytes 393232 | tf_op jit(solution)/shard_map/psum | solution.py:114
  523.0 0.9 dynamic-slice_divide_fusion.1
  523.9 0.7 copy.36
  (59 shorter events, 10.5 us)
Async XLA Ops:
  8.5 80.6 %copy-start.1 = (s32[4096,2]{0,1:T(2,128)S(1)}, s32[4096,2]{0,1:T(2,128)}, u32[]{:S(2)}) copy-start(s32[4096,2]{0,1:T(2,128)} %param.10) | copy-start | bytes 98308
  8.5 80.6 %copy-start.2 = (s32[4096]{0:T(1024)S(1)}, s32[4096]{0:T(1024)}, u32[]{:S(2)}) copy-start(s32[4096]{0:T(1024)} %param.11) | copy-start | bytes 49156
  81.0 14.6 %all-to-all-start = ((s32[32,1,256]{2,1,0:T(1,128)}), s32[32,1,256]{2,1,0:T(1,128)S(1)}, u32[]{:S(2)}, u32[]{:S(2)}) async-start(s32[32,1,256]{2,1,0:T(1,128)} %bitcast.7), calls=%async_computation | async-start | bytes 65536 | tf_op jit(solution)/shard_map/all_to_all | solution.py:62
  88.3 353.6 %all-gather.2.cloned.1.call-start = ((), (), s32[]{:S(2)}) async-start(), calls=%async_computation.2 | async-start | bytes 1081344 | tf_op jit(solution)/shard_map/all_gather | solution.py:79
  95.5 353.7 %all-to-all-start.1 = ((bf16[32,256,128]{1,2,0:T(8,128)(2,1)}), bf16[32,256,128]{1,2,0:T(8,128)(2,1)}, u32[]{:S(2)}, u32[]{:S(2)}) async-start(bf16[32,256,128]{1,2,0:T(8,128)(2,1)} %copy.33), calls=%async_computation.1 | async-start | bytes 4194304 | tf_op jit(solution)/shard_map/all_to_all | solution.py:55
  99.8 423.2 %all-reduce.3.cloned.1.call-start = ((), (), s32[]{:S(2)}) async-start(), calls=%async_computation.3 | async-start | bytes 786432 | tf_op jit(solution)/shard_map/psum | solution.py:114
  449.2 2.8 copy-start
Sparse Core Ops, SparseCore 0:
  92.0 64.4 all-gather.1
  465.0 57.9 all-reduce.2
where the time goes:
time: 535 us; the launch traced here: 531 us
  local copies, waits for them, and re-layouts  339 us (63%)
  matrix products  69.2 us (13%)
  waiting for transfers between devices  60.6 us (11%)
  other arithmetic  27 us (5%)
  between operations  13.7 us (3%)
  starting transfers between devices  11.8 us (2%)
  loops' own time  10.1 us (2%)
    gather x2, local copies, waits for them, and re-layouts, local(): jnp.take(model_vis.reshape(row_block * col_block, width), first * col_blo...  288 us
    psum x1, waiting for transfers between devices, local(): numer, denom = lax.psum((numer, denom), 'acol')  58.1 us
    dot_general x16, matrix products, place(): jnp.dot(table, row_data, preferred_element_type=jnp.float32)  39.3 us
    gather x1, local copies, waits for them, and re-layouts, local(): found = jnp.take(slot_info, safe, axis=0)  27.7 us
    dot_general x16, matrix products, place(): tagged = jnp.dot(table, codes, preferred_element_type=jnp.float32)  12.7 us
  transfers between devices with their start and end apart: 4, of which 2 were waited for; matrix products, arithmetic and copies ran while one was open for 67% of the time, Pallas kernels for 0%

commit v1 on v0

v1 whole, which is shorter than its diff:
```python
import functools

import jax
import jax.numpy as jnp
from jax import lax
from jax.experimental import pallas as pl
from jax.experimental.pallas import tpu as pltpu
from jax.sharding import PartitionSpec as P

RIDGE = 1.0
LANES = 128
MESH = pl.DeviceIdType.MESH


def rows_at(ref, start, count):
    return ref[pl.ds(start, count), :]


def route_kernel(
    devices, capacity, slots, rows_ref, base_ref, out_ref, label_ref,
    wide, spread, target, local_id, empty, target_s, local_s, sems,
):
    blocks = base_ref.shape[0]
    count = rows_ref.shape[0]
    empty[...] = jnp.full(empty.shape, slots, jnp.int32)
    fill = pltpu.make_async_copy(empty, label_ref, sems.at[0])
    fill.start()
    order = lax.broadcasted_iota(jnp.int32, (LANES, LANES), 0)
    upper = (order < lax.broadcasted_iota(jnp.int32, (LANES, LANES), 1)).astype(jnp.bfloat16)
    tile = lax.broadcasted_iota(jnp.int32, (devices, LANES), 0)
    before = jnp.zeros((devices, 1), jnp.float32)
    for block in range(blocks):
        slot = base_ref[block : block + 1, :]
        owner = slot // slots
        hit = tile == owner
        hits = jnp.where(hit, 1.0, 0.0)
        within = jnp.dot(hits.astype(jnp.bfloat16), upper, preferred_element_type=jnp.float32)
        ranking = jnp.sum(jnp.where(hit, within + before, 0.0), axis=0, keepdims=True)
        before = before + jnp.sum(hits, axis=1, keepdims=True)
        target[block : block + 1, :] = owner * capacity + ranking.astype(jnp.int32)
        local_id[block : block + 1, :] = slot - owner * slots
    to_target = pltpu.make_async_copy(target, target_s, sems.at[1])
    to_target.start()
    to_local = pltpu.make_async_copy(local_id, local_s, sems.at[2])
    to_local.start()
    wide[...] = rows_ref[...].astype(jnp.float32)
    spread[...] = jnp.zeros_like(spread)
    to_target.wait()
    to_local.wait()
    fill.wait()

    def place_block(block, carry):
        def place(at, carry):
            spot = target_s[block, at]
            label_ref[spot] = local_s[block, at]
            spread[pl.ds(spot, 1), :] = wide[pl.ds(block * LANES + at, 1), :]
            return carry

        return lax.fori_loop(0, LANES, place, carry, unroll=16)

    lax.fori_loop(0, count // LANES, place_block, 0)
    out_ref[...] = spread[...].astype(jnp.bfloat16)


def route(rows, baseline, devices, capacity, slots):
    count, width = rows.shape
    blocks = count // LANES
    total = devices * capacity
    return pl.pallas_call(
        functools.partial(route_kernel, devices, capacity, slots),
        out_shape=(
            jax.ShapeDtypeStruct((total, width), jnp.bfloat16),
            jax.ShapeDtypeStruct((total,), jnp.int32),
        ),
        in_specs=[pl.BlockSpec(memory_space=pltpu.VMEM)] * 2,
        out_specs=(
            pl.BlockSpec(memory_space=pltpu.VMEM),
            pl.BlockSpec(memory_space=pltpu.SMEM),
        ),
        scratch_shapes=[
            pltpu.VMEM((count, width), jnp.float32),
            pltpu.VMEM((total, width), jnp.float32),
            pltpu.VMEM((blocks, LANES), jnp.int32),
            pltpu.VMEM((blocks, LANES), jnp.int32),
            pltpu.VMEM((total,), jnp.int32),
            pltpu.SMEM((blocks, LANES), jnp.int32),
            pltpu.SMEM((blocks, LANES), jnp.int32),
            pltpu.SemaphoreType.DMA((3,)),
        ],
        name="route",
    )(rows, baseline.reshape(blocks, LANES))


def share_kernel(
    row_count, col_count, label_ref, gain_ref, name_ref, column_ref,
    send_sem, recv_sem, gain_send, gain_recv, local_sem,
):
    devices = row_count * col_count
    my_row = lax.axis_index("arow")
    my_col = lax.axis_index("acol")
    me = my_row * col_count + my_col
    barrier = pltpu.get_barrier_semaphore()

    def place(index):
        return (index // col_count, lax.rem(index, col_count))

    def greet(step, carry):
        pl.semaphore_signal(
            barrier, inc=1, device_id=place(lax.rem(me + step, devices)), device_id_type=MESH
        )
        return carry

    lax.fori_loop(1, devices, greet, 0)
    own = pltpu.make_async_copy(label_ref.at[me], name_ref.at[me], local_sem.at[0])
    own.start()
    pl.semaphore_wait(barrier, devices - 1)

    def label_copy(to, slot):
        return pltpu.make_async_remote_copy(
            src_ref=label_ref.at[to],
            dst_ref=name_ref.at[slot],
            send_sem=send_sem.at[to],
            recv_sem=recv_sem.at[slot],
            device_id=place(to),
            device_id_type=MESH,
        )

    def send(step, carry):
        label_copy(lax.rem(me + step, devices), me).start()
        return carry

    lax.fori_loop(1, devices, send, 0)
    column = me // row_count
    part = lax.rem(me, row_count)

    def gain_copy(row, col, slot):
        return pltpu.make_async_remote_copy(
            src_ref=gain_ref,
            dst_ref=column_ref.at[slot],
            send_sem=gain_send.at[row],
            recv_sem=gain_recv.at[slot],
            device_id=(row, col),
            device_id_type=MESH,
        )

    own_gain = pltpu.make_async_copy(gain_ref, column_ref.at[part], local_sem.at[1])
    for row in range(row_count):
        stays = jnp.logical_and(row == my_row, column == my_col)

        @pl.when(jnp.logical_not(stays))
        def _():
            gain_copy(row, column, part).start()

        @pl.when(stays)
        def _():
            own_gain.start()

    for row in range(row_count):
        stays = jnp.logical_and(row == my_row, column == my_col)

        @pl.when(jnp.logical_not(stays))
        def _():
            gain_copy(row, column, part).wait_send()

        @pl.when(stays)
        def _():
            own_gain.wait()

    for slot in range(row_count):
        source = my_col * row_count + slot

        @pl.when(source != me)
        def _():
            gain_copy(0, my_col, slot).wait_recv()

    def finish(step, carry):
        other = lax.rem(me + step, devices)
        label_copy(other, other).wait()
        return carry

    lax.fori_loop(1, devices, finish, 0)
    own.wait()


def share(labels, gains, row_count, col_count):
    devices = row_count * col_count
    return pl.pallas_call(
        functools.partial(share_kernel, row_count, col_count),
        out_shape=(
            jax.ShapeDtypeStruct(labels.shape, jnp.int32),
            jax.ShapeDtypeStruct((row_count,) + gains.shape, jnp.float32),
        ),
        in_specs=[pl.BlockSpec(memory_space=pltpu.VMEM)] * 2,
        out_specs=(pl.BlockSpec(memory_space=pltpu.VMEM),) * 2,
        scratch_shapes=[
            pltpu.SemaphoreType.DMA((devices,)),
            pltpu.SemaphoreType.DMA((devices,)),
            pltpu.SemaphoreType.DMA((row_count,)),
            pltpu.SemaphoreType.DMA((row_count,)),
            pltpu.SemaphoreType.DMA((2,)),
        ],
        compiler_params=pltpu.CompilerParams(collective_id=0, has_side_effects=True),
        name="share",
    )(labels, gains)


def gather_kernel(
    col_block, pairs, chunk, name_ref, table_ref, model_ref, gain_ref, c_ref, info_ref,
    model, gain_rows, picked, sem,
):
    total = c_ref.shape[0]
    width = c_ref.shape[1]
    half = width // 2
    load = pltpu.make_async_copy(model_ref, model, sem)
    load.start()

    def look(at, carry):
        info = table_ref[name_ref[at]]
        info_ref[at] = info
        second = info & (col_block - 1)
        gain_rows[pl.ds(at, 1), :] = gain_ref[pl.ds(second, 1), :]
        return carry

    lax.fori_loop(0, total, look, 0, unroll=16)
    load.wait()

    def piece(number, carry):
        start = number * chunk

        def fetch(at, carry):
            info = info_ref[start + at]
            spot = (info >> 1) & (pairs - 1)
            picked[pl.ds(2 * at + 1 - (info & 1), 2), :] = model[spot].astype(jnp.float32)
            return carry

        lax.fori_loop(0, chunk, fetch, 0, unroll=16)
        m = picked[pl.ds(1, chunk, stride=2), :]
        g = gain_rows[pl.ds(pl.multiple_of(start, chunk), chunk), :]
        a = m * g
        b = m * pltpu.roll(g, half, 1)
        low = lax.broadcasted_iota(jnp.int32, (chunk, width), 1) < half
        c_ref[pl.ds(pl.multiple_of(start, chunk), chunk), :] = jnp.where(
            low, a + pltpu.roll(a, half, 1), pltpu.roll(b, half, 1) - b
        )
        return carry

    lax.fori_loop(0, total // chunk, piece, 0)


def gather(names, table, model_vis, column_gains):
    row_block, col_block, width = model_vis.shape
    pairs = row_block * col_block // 2
    total = names.shape[0]
    chunk = min(512, total)
    return pl.pallas_call(
        functools.partial(gather_kernel, col_block, pairs, chunk),
        out_shape=(
            jax.ShapeDtypeStruct((total, width), jnp.float32),
            jax.ShapeDtypeStruct((total,), jnp.int32),
        ),
        in_specs=[
            pl.BlockSpec(memory_space=pltpu.SMEM),
            pl.BlockSpec(memory_space=pltpu.SMEM),
            pl.BlockSpec(memory_space=pl.ANY),
            pl.BlockSpec(memory_space=pltpu.VMEM),
        ],
        out_specs=(
            pl.BlockSpec(memory_space=pltpu.VMEM),
            pl.BlockSpec(memory_space=pltpu.SMEM),
        ),
        scratch_shapes=[
            pltpu.VMEM((pairs, 2, width), jnp.bfloat16),
            pltpu.VMEM((total, width), jnp.float32),
            pltpu.VMEM((2 * chunk + 8, width), jnp.float32),
            pltpu.SemaphoreType.DMA,
        ],
        compiler_params=pltpu.CompilerParams(vmem_limit_bytes=56 << 20),
        cost_estimate=pl.CostEstimate(
            flops=1 << 20, bytes_accessed=model_vis.size * 2, transcendentals=0
        ),
        name="gather",
    )(names, table, model_vis.reshape(pairs, 2, width), column_gains)


def pick_rows(info, row_block, col_block):
    first = (info // col_block) & (row_block - 1)
    weight = (info // (row_block * col_block)).astype(jnp.float32)
    spots = lax.broadcasted_iota(jnp.int32, (row_block, info.shape[1]), 0)
    return jnp.where(spots == first, weight, 0.0).astype(jnp.bfloat16)


def power_kernel(col_block, info_ref, c_ref, out_ref):
    row_block, width = out_ref.shape
    half = width // 2

    @pl.when(pl.program_id(0) == 0)
    def _():
        out_ref[...] = jnp.zeros_like(out_ref)

    c = c_ref[...]
    power = c * c
    power = power + pltpu.roll(power, half, 1)
    high = power.astype(jnp.bfloat16).astype(jnp.float32)
    low = lax.broadcasted_iota(jnp.int32, power.shape, 1) < half
    values = jnp.where(low, high, power - high).astype(jnp.bfloat16)
    sums = jnp.dot(
        pick_rows(info_ref[0], row_block, col_block), values, preferred_element_type=jnp.float32
    )
    out_ref[...] += sums + pltpu.roll(sums, half, 1)


def product_kernel(col_block, info_ref, c_ref, rows_ref, out_ref):
    row_block, width = out_ref.shape
    half = width // 2

    @pl.when(pl.program_id(0) == 0)
    def _():
        out_ref[...] = jnp.zeros_like(out_ref)

    c = c_ref[...]
    r = rows_ref[...].astype(jnp.float32)
    a = c * r
    b = c * pltpu.roll(r, half, 1)
    low = lax.broadcasted_iota(jnp.int32, c.shape, 1) < half
    product = jnp.where(low, a - pltpu.roll(a, half, 1), b + pltpu.roll(b, half, 1))
    high = product.astype(jnp.bfloat16)
    rest = (product - high.astype(jnp.float32)).astype(jnp.bfloat16)
    values = jnp.concatenate([high, rest], axis=1)
    sums = jnp.dot(
        pick_rows(info_ref[0], row_block, col_block), values, preferred_element_type=jnp.float32
    )
    out_ref[...] += sums[:, :width] + sums[:, width:]


def segment(kernel, name, info, arrays, row_block, col_block):
    total, width = arrays[0].shape
    chunk = min(1024, total)
    steps = total // chunk
    return pl.pallas_call(
        functools.partial(kernel, col_block),
        out_shape=jax.ShapeDtypeStruct((row_block, width), jnp.float32),
        grid=(steps,),
        in_specs=[pl.BlockSpec((1, 1, chunk), lambda i: (i, 0, 0))]
        + [pl.BlockSpec((chunk, width), lambda i: (i, 0))] * len(arrays),
        out_specs=pl.BlockSpec((row_block, width), lambda i: (0, 0)),
        cost_estimate=pl.CostEstimate(
            flops=2 * row_block * total * 2 * width,
            bytes_accessed=total * width * 4,
            transcendentals=0,
        ),
        name=name,
    )(info.reshape(steps, 1, chunk), *arrays)


def collect_kernel(count, divided, *refs):
    if divided:
        part_ref, den_ref, out_ref, held, send_sem, recv_sem = refs
    else:
        part_ref, out_ref, held, send_sem, recv_sem = refs
    me = lax.axis_index("acol")
    barrier = pltpu.get_barrier_semaphore()
    for step in range(1, count):
        pl.semaphore_signal(
            barrier,
            inc=1,
            device_id=(lax.axis_index("arow"), lax.rem(me + step, count)),
            device_id_type=MESH,
        )
    pl.semaphore_wait(barrier, count - 1)

    def copy(to, slot):
        return pltpu.make_async_remote_copy(
            src_ref=part_ref.at[to],
            dst_ref=held.at[slot],
            send_sem=send_sem.at[to],
            recv_sem=recv_sem.at[slot],
            device_id=(lax.axis_index("arow"), to),
            device_id_type=MESH,
        )

    for step in range(1, count):
        copy(lax.rem(me + step, count), me).start()
    total = part_ref[me]
    for step in range(1, count):
        other = lax.rem(me + step, count)
        copy(other, other).wait()
        total = total + held[other]
    if divided:
        total = total / (den_ref[...] + RIDGE)
    out_ref[...] = total


def collect(parts, denominator, count, number):
    rows, width = parts.shape
    share_rows = rows // count
    divided = denominator is not None
    operands = [parts.reshape(count, share_rows, width)] + ([denominator] if divided else [])
    return pl.pallas_call(
        functools.partial(collect_kernel, count, divided),
        out_shape=jax.ShapeDtypeStruct((share_rows, width), jnp.float32),
        in_specs=[pl.BlockSpec(memory_space=pltpu.VMEM)] * len(operands),
        out_specs=pl.BlockSpec(memory_space=pltpu.VMEM),
        scratch_shapes=[
            pltpu.VMEM((count, share_rows, width), jnp.float32),
            pltpu.SemaphoreType.DMA((count,)),
            pltpu.SemaphoreType.DMA((count,)),
        ],
        compiler_params=pltpu.CompilerParams(collective_id=number, has_side_effects=True),
        name="collect" + str(number),
    )(*operands)


def local(row_count, col_count, row_data, row_baseline, pair_table, lengths, model_vis, gains):
    devices = row_count * col_count
    slots = lengths.shape[0]
    capacity = 4 * row_data.shape[0] // devices
    row_block, col_block, width = model_vis.shape
    total = devices * capacity
    my_row = lax.axis_index("arow")
    my_col = lax.axis_index("acol")
    first = pair_table[:, 0] - my_row * row_block
    second = pair_table[:, 1] - my_col * col_block
    table = (lengths * row_block + first) * col_block + second
    table = jnp.concatenate([table, jnp.zeros((LANES,), jnp.int32)])
    outgoing, labels = route(row_data, row_baseline, devices, capacity, slots)
    names, column_gains = share(
        labels.reshape(devices, 1, capacity), gains, row_count, col_count
    )
    outgoing, names = lax.optimization_barrier((outgoing, names))
    arrived = lax.all_to_all(
        outgoing.reshape(devices, capacity, width),
        ("arow", "acol"),
        split_axis=0,
        concat_axis=0,
        tiled=True,
    ).reshape(total, width)
    c, info = gather(
        names.reshape(total), table, model_vis, column_gains.reshape(col_block, width)
    )
    power = segment(power_kernel, "power", info, [c], row_block, col_block)
    denominator = collect(power, None, col_count, 1)
    product = segment(product_kernel, "product", info, [c, arrived], row_block, col_block)
    return collect(product, denominator, col_count, 2)


def solution(mesh):
    placed = (
        P(("arow", "acol"), None),
        P(("arow", "acol")),
        P(("arow", "acol"), None),
        P(("arow", "acol")),
        P("arow", "acol", None),
        P(("arow", "acol"), None),
    )
    return jax.shard_map(
        functools.partial(local, mesh.shape["arow"], mesh.shape["acol"]),
        mesh=mesh,
        in_specs=placed,
        out_specs=P(("arow", "acol"), None),
        check_vma=False,
    )
```

time: 535 us -> 120 us (0.22)
  local copies, waits for them, and re-layouts: 339 us -> 3.3 us
  Pallas kernels: 0 us -> 110 us
  matrix products: 69.2 us -> 0 us
  waiting for transfers between devices: 60.6 us -> 0.01 us
  other arithmetic: 27 us -> 0.03 us
  between operations: 13.7 us -> 0.1 us
  loops' own time: 10.1 us -> 0 us
  starting transfers between devices: 11.8 us -> 5.59 us
    gather x3 -> x0, local copies, waits for them, and re-layouts: 316 us -> none  [the longest x2 288 us: local(): jnp.take(model_vis.reshape(row_block * col_block, width), first * col_blo...]
    pallas_call x0 -> x7, Pallas kernels: none -> 110 us  [the longest x1 52.6 us: gather(): pl.pallas_call(functools.partial(gather_kernel, col_block, pairs, chunk),...]
    dot_general x35 -> x0, matrix products: 69.2 us -> none  [the longest x16 39.3 us: place(): jnp.dot(table, row_data, preferred_element_type=jnp.float32)]
    psum x1 -> x0, waiting for transfers between devices: 58.1 us -> none  [local(): numer, denom = lax.psum((numer, denom), 'acol')]
    select_n x4 -> x0, other arithmetic: 16.3 us -> none  [the longest x2 9.56 us: local(): found = jnp.take(slot_info, safe, axis=0)]
    another operation x1 -> x0, loops' own time: 10.1 us -> none  [local(): outgoing, tags = lax.map(place, jnp.arange(groups, dtype=jnp.int32))]
    dynamic_slice x16 -> x0, local copies, waits for them, and re-layouts: 9.55 us -> none  [local(): outgoing, tags = lax.map(place, jnp.arange(groups, dtype=jnp.int32))]
    all_to_all x1 -> x0, starting transfers between devices: 7.32 us -> none  [local(): lax.all_to_all(labels.reshape(devices, capacity), ('arow', 'acol'), split...]
  transfers between devices with their start and end apart: 4 -> 1, of which waited for: 2 -> 0; matrix products, arithmetic and copies ran while one was open for 67% -> 1% of each run, Pallas kernels for 0% -> 58%
where the time goes in v1:
time: 120 us; the launch traced here: 119 us
  Pallas kernels  110 us (92%)
  starting transfers between devices  5.59 us (5%)
  local copies, waits for them, and re-layouts  3.3 us (3%)
    pallas_call x1, Pallas kernels, gather(): pl.pallas_call(functools.partial(gather_kernel, col_block, pairs, chunk),...  52.6 us
    pallas_call x2, Pallas kernels, segment(): pl.pallas_call(functools.partial(kernel, col_block), out_shape=jax.ShapeD...  17.5 us
    pallas_call x2, Pallas kernels, collect(): pl.pallas_call(functools.partial(collect_kernel, count, divided), out_sha...  16.5 us
    pallas_call x1, Pallas kernels, share(): pl.pallas_call(functools.partial(share_kernel, row_count, col_count), out...  12.5 us
    pallas_call x1, Pallas kernels, route(): pl.pallas_call(functools.partial(route_kernel, devices, capacity, slots),...  10.9 us
    all_to_all x1, starting transfers between devices, local(): lax.all_to_all(outgoing.reshape(devices, capacity, width), ('arow', 'acol...  5.59 us
    unnamed x7, local copies, waits for them, and re-layouts  2.7 us
  transfers between devices with their start and end apart: 1, of which 0 were waited for; matrix products, arithmetic and copies ran while one was open for 1% of the time, Pallas kernels for 58%

profile of v1, /device:TPU:0, one launch (start us, length us, event | category | flops | bytes accessed | tf_op | source)
XLA Modules:
  0.0 119.0 jit_solution(3262527421938376828)
XLA Ops:
  0.0 0.0 copy-start.1
  0.0 0.0 copy-start.2
  0.0 10.9 %route.1 = (bf16[8192,128]{1,0:T(8,128)(2,1)}, s32[8192]{0:T(1024)}) custom-call(bf16[2048,128]{1,0:T(8,128)(2,1)} %rows_ref.1, s32[16,128]{1,0:T(8,128)} %bitcast.22), custom_call_target="tpu_custom_call" | custom-call | tf_op jit(solution)/shard_map/route/pallas_call | solution.py:69
  11.0 12.5 %share.1 = (s32[32,1,256]{2,1,0:T(1,128)}, f32[4,64,128]{2,1,0:T(8,128)}) custom-call(s32[32,1,256]{2,1,0:T(1,128)} %bitcast.21, f32[64,128]{1,0:T(8,128)} %gain_ref.1), custom_call_target="tpu_custom_call" | custom-call | tf_op jit(solution)/shard_map/share/pallas_call | solution.py:187
  23.5 5.6 %all-to-all-start = ((bf16[32,256,128]{2,1,0:T(8,128)(2,1)}), bf16[32,256,128]{2,1,0:T(8,128)(2,1)S(1)}, u32[]{:S(2)}, u32[]{:S(2)}) async-start(bf16[32,256,128]{2,1,0:T(8,128)(2,1)} %bitcast.13), calls=%async_computation | async-start | bytes 4194304 | tf_op jit(solution)/shard_map/all_to_all | solution.py:430
  29.1 0.0 copy-done.1
  29.1 0.0 copy-done.2
  29.2 0.6 concatenate.3.table_ref
  29.8 52.6 %gather.1 = (f32[8192,128]{1,0:T(8,128)}, s32[8192]{0:T(1024)}) custom-call(s32[8192]{0:T(1024)} %bitcast.20, s32[4224]{0:T(1024)} %concatenate.3.table_ref, bf16[65536,2,128]{2,1,0:T(2,128)(2,1)} %bitcast.12, f32[256,128]{1,0:T(8,128)} %bitcast.17), custom_call_target="tpu_custom_call" | custom-call | flops 1048576 | bytes 33554432 | tf_op jit(solution)/shard_map/gather/pallas_call | solution.py:255
  82.3 8.2 %power.1 = f32[512,128]{1,0:T(8,128)} custom-call(s32[8,1,1024]{2,1,0:T(1,128)} %bitcast.23, f32[8192,128]{1,0:T(8,128)} %get-tuple-element.19.c_ref), custom_call_target="tpu_custom_call" | custom-call | flops 2147483648 | bytes 4194304 | tf_op jit(solution)/shard_map/power/pallas_call | solution.py:339
  90.6 8.4 %collect1.1.refs_1_ = f32[64,128]{1,0:T(8,128)} custom-call(f32[8,64,128]{2,1,0:T(8,128)} %bitcast.16), custom_call_target="tpu_custom_call" | custom-call | tf_op jit(solution)/shard_map/collect1/pallas_call | solution.py:398
  99.0 0.0 all-to-all-done
  99.0 0.0 copy-start
  99.0 1.3 %copy-done = bf16[32,256,128]{2,1,0:T(8,128)(2,1)} copy-done((bf16[32,256,128]{2,1,0:T(8,128)(2,1)}, bf16[32,256,128]{2,1,0:T(8,128)(2,1)S(1)}, u32[]{:S(2)}) %copy-start) | copy-done | bytes 2097176
  100.3 9.2 %product.1 = f32[512,128]{1,0:T(8,128)} custom-call(s32[8,1,1024]{2,1,0:T(1,128)} %bitcast.24, f32[8192,128]{1,0:T(8,128)} %get-tuple-element.19.c_ref, bf16[8192,128]{1,0:T(8,128)(2,1)} %bitcast.14), custom_call_target="tpu_custom_call" | custom-call | flops 2147483648 | bytes 4194304 | tf_op jit(solution)/shard_map/product/pallas_call | solution.py:339
  109.5 8.1 %collect2.1 = f32[64,128]{1,0:T(8,128)} custom-call(f32[8,64,128]{2,1,0:T(8,128)} %bitcast.15, f32[64,128]{1,0:T(8,128)} %collect1.1.refs_1_), custom_call_target="tpu_custom_call" | custom-call | tf_op jit(solution)/shard_map/collect2/pallas_call | solution.py:398
  117.6 1.4 %copy.8 = f32[64,128]{1,0:T(8,128)} copy(f32[64,128]{1,0:T(8,128)} %collect2.1) | data formatting | bytes 65536
  (2 shorter events, 0.0 us)
Async XLA Ops:
  0.0 29.1 %copy-start.1 = (s32[4096,2]{0,1:T(2,128)S(1)}, s32[4096,2]{0,1:T(2,128)}, u32[]{:S(2)}) copy-start(s32[4096,2]{0,1:T(2,128)} %param.8) | copy-start | bytes 98308
  0.0 29.1 %copy-start.2 = (s32[4096]{0:T(1024)S(1)}, s32[4096]{0:T(1024)}, u32[]{:S(2)}) copy-start(s32[4096]{0:T(1024)} %param.9) | copy-start | bytes 49156
  23.5 75.5 %all-to-all-start = ((bf16[32,256,128]{2,1,0:T(8,128)(2,1)}), bf16[32,256,128]{2,1,0:T(8,128)(2,1)S(1)}, u32[]{:S(2)}, u32[]{:S(2)}) async-start(bf16[32,256,128]{2,1,0:T(8,128)(2,1)} %bitcast.13), calls=%async_computation | async-start | bytes 4194304 | tf_op jit(solution)/shard_map/all_to_all | solution.py:430
  99.0 1.3 %copy-start = (bf16[32,256,128]{2,1,0:T(8,128)(2,1)}, bf16[32,256,128]{2,1,0:T(8,128)(2,1)S(1)}, u32[]{:S(2)}) copy-start(bf16[32,256,128]{2,1,0:T(8,128)(2,1)S(1)} %all-to-all-done) | copy-start | bytes 6291460

commit v2 on v1

--- a/solution.py
+++ b/solution.py
@@ -9,6 +9,8 @@
 
 RIDGE = 1.0
 LANES = 128
+GROUP = 32
+WEIGHT_BITS = 4
 MESH = pl.DeviceIdType.MESH
 
 
@@ -50,13 +52,19 @@
     fill.wait()
 
     def place_block(block, carry):
-        def place(at, carry):
-            spot = target_s[block, at]
-            label_ref[spot] = local_s[block, at]
-            spread[pl.ds(spot, 1), :] = wide[pl.ds(block * LANES + at, 1), :]
+        def place(group, carry):
+            first = group * GROUP
+            spots = [target_s[block, first + k] for k in range(GROUP)]
+            ids = [local_s[block, first + k] for k in range(GROUP)]
+            held = [
+                wide[pl.ds(block * LANES + first + k, 1), :] for k in range(GROUP)
+            ]
+            for k in range(GROUP):
+                label_ref[spots[k]] = ids[k]
+                spread[pl.ds(spots[k], 1), :] = held[k]
             return carry
 
-        return lax.fori_loop(0, LANES, place, carry, unroll=16)
+        return lax.fori_loop(0, LANES // GROUP, place, carry)
 
     lax.fori_loop(0, count // LANES, place_block, 0)
     out_ref[...] = spread[...].astype(jnp.bfloat16)
@@ -205,39 +213,51 @@
 
 
 def gather_kernel(
-    col_block, pairs, chunk, name_ref, table_ref, model_ref, gain_ref, c_ref, info_ref,
-    model, gain_rows, picked, sem,
+    col_block, chunk, name_ref, table_ref, model_ref, gain_ref, c_ref, info_ref,
+    model, pair_gain, gain_rows, picked, sem,
 ):
     total = c_ref.shape[0]
     width = c_ref.shape[1]
     half = width // 2
     load = pltpu.make_async_copy(model_ref, model, sem)
     load.start()
-
-    def look(at, carry):
-        info = table_ref[name_ref[at]]
-        info_ref[at] = info
-        second = info & (col_block - 1)
-        gain_rows[pl.ds(at, 1), :] = gain_ref[pl.ds(second, 1), :]
+    shift = col_block.bit_length() + WEIGHT_BITS
+    odd = lax.broadcasted_iota(jnp.int32, gain_ref.shape, 0) & 1
+    pair_gain[pl.ds(0, col_block, stride=2), :] = jnp.where(odd == 0, gain_ref[...], 0.0)
+    pair_gain[pl.ds(1, col_block, stride=2), :] = jnp.where(odd == 1, gain_ref[...], 0.0)
+
+    def look(group, carry):
+        first = group * GROUP
+        names = [name_ref[first + k] for k in range(GROUP)]
+        infos = [table_ref[name] for name in names]
+        held = [pair_gain[pl.ds(info & (2 * col_block - 1), 2), :] for info in infos]
+        for k in range(GROUP):
+            info_ref[first + k] = infos[k]
+            gain_rows[pl.ds(2 * (first + k), 2), :] = held[k]
         return carry
 
-    lax.fori_loop(0, total, look, 0, unroll=16)
+    lax.fori_loop(0, total // GROUP, look, 0)
     load.wait()
 
     def piece(number, carry):
         start = number * chunk
 
-        def fetch(at, carry):
-            info = info_ref[start + at]
-            spot = (info >> 1) & (pairs - 1)
-            picked[pl.ds(2 * at + 1 - (info & 1), 2), :] = model[spot].astype(jnp.float32)
+        def fetch(group, carry):
+            first = group * GROUP
+            infos = [info_ref[start + first + k] for k in range(GROUP)]
+            held = [model[info >> shift].astype(jnp.float32) for info in infos]
+            for k in range(GROUP):
+                picked[pl.ds(2 * (first + k), 2), :] = held[k]
             return carry
 
-        lax.fori_loop(0, chunk, fetch, 0, unroll=16)
-        m = picked[pl.ds(1, chunk, stride=2), :]
-        g = gain_rows[pl.ds(pl.multiple_of(start, chunk), chunk), :]
-        a = m * g
-        b = m * pltpu.roll(g, half, 1)
+        lax.fori_loop(0, chunk // GROUP, fetch, 0)
+        at = pl.multiple_of(2 * start, 2 * chunk)
+        m_even = picked[pl.ds(0, chunk, stride=2), :]
+        m_odd = picked[pl.ds(1, chunk, stride=2), :]
+        g_even = gain_rows[pl.ds(at, chunk, stride=2), :]
+        g_odd = gain_rows[pl.ds(at + 1, chunk, stride=2), :]
+        a = m_even * g_even + m_odd * g_odd
+        b = m_even * pltpu.roll(g_even, half, 1) + m_odd * pltpu.roll(g_odd, half, 1)
         low = lax.broadcasted_iota(jnp.int32, (chunk, width), 1) < half
         c_ref[pl.ds(pl.multiple_of(start, chunk), chunk), :] = jnp.where(
             low, a + pltpu.roll(a, half, 1), pltpu.roll(b, half, 1) - b
@@ -253,7 +273,7 @@
     total = names.shape[0]
     chunk = min(512, total)
     return pl.pallas_call(
-        functools.partial(gather_kernel, col_block, pairs, chunk),
+        functools.partial(gather_kernel, col_block, chunk),
         out_shape=(
             jax.ShapeDtypeStruct((total, width), jnp.float32),
             jax.ShapeDtypeStruct((total,), jnp.int32),
@@ -270,8 +290,9 @@
         ),
         scratch_shapes=[
             pltpu.VMEM((pairs, 2, width), jnp.bfloat16),
-            pltpu.VMEM((total, width), jnp.float32),
-            pltpu.VMEM((2 * chunk + 8, width), jnp.float32),
+            pltpu.VMEM((2 * col_block, width), jnp.float32),
+            pltpu.VMEM((2 * total, width), jnp.float32),
+            pltpu.VMEM((2 * chunk, width), jnp.float32),
             pltpu.SemaphoreType.DMA,
         ],
         compiler_params=pltpu.CompilerParams(vmem_limit_bytes=56 << 20),
@@ -283,8 +304,9 @@
 
 
 def pick_rows(info, row_block, col_block):
-    first = (info // col_block) & (row_block - 1)
-    weight = (info // (row_block * col_block)).astype(jnp.float32)
+    column_bits = col_block.bit_length()
+    first = info >> (2 * column_bits + WEIGHT_BITS - 2)
+    weight = ((info >> column_bits) & ((1 << WEIGHT_BITS) - 1)).astype(jnp.float32)
     spots = lax.broadcasted_iota(jnp.int32, (row_block, info.shape[1]), 0)
     return jnp.where(spots == first, weight, 0.0).astype(jnp.bfloat16)
 
@@ -352,11 +374,9 @@
     )(info.reshape(steps, 1, chunk), *arrays)
 
 
-def collect_kernel(count, divided, *refs):
-    if divided:
-        part_ref, den_ref, out_ref, held, send_sem, recv_sem = refs
-    else:
-        part_ref, out_ref, held, send_sem, recv_sem = refs
+def collect_kernel(
+    count, num_ref, den_ref, out_ref, num_held, den_held, num_send, num_recv, den_send, den_recv
+):
     me = lax.axis_index("acol")
     barrier = pltpu.get_barrier_semaphore()
     for step in range(1, count):
@@ -368,46 +388,50 @@
         )
     pl.semaphore_wait(barrier, count - 1)
 
-    def copy(to, slot):
-        return pltpu.make_async_remote_copy(
-            src_ref=part_ref.at[to],
-            dst_ref=held.at[slot],
-            send_sem=send_sem.at[to],
-            recv_sem=recv_sem.at[slot],
-            device_id=(lax.axis_index("arow"), to),
-            device_id_type=MESH,
-        )
+    def copies(to, slot):
+        return [
+            pltpu.make_async_remote_copy(
+                src_ref=part.at[to],
+                dst_ref=held.at[slot],
+                send_sem=send.at[to],
+                recv_sem=recv.at[slot],
+                device_id=(lax.axis_index("arow"), to),
+                device_id_type=MESH,
+            )
+            for part, held, send, recv in (
+                (den_ref, den_held, den_send, den_recv),
+                (num_ref, num_held, num_send, num_recv),
+            )
+        ]
 
     for step in range(1, count):
-        copy(lax.rem(me + step, count), me).start()
-    total = part_ref[me]
+        for copy in copies(lax.rem(me + step, count), me):
+            copy.start()
+    num = num_ref[me]
+    den = den_ref[me]
     for step in range(1, count):
         other = lax.rem(me + step, count)
-        copy(other, other).wait()
-        total = total + held[other]
-    if divided:
-        total = total / (den_ref[...] + RIDGE)
-    out_ref[...] = total
-
-
-def collect(parts, denominator, count, number):
-    rows, width = parts.shape
+        for copy in copies(other, other):
+            copy.wait()
+        num = num + num_held[other]
+        den = den + den_held[other]
+    out_ref[...] = num / (den + RIDGE)
+
+
+def collect(numerator, denominator, count):
+    rows, width = numerator.shape
     share_rows = rows // count
-    divided = denominator is not None
-    operands = [parts.reshape(count, share_rows, width)] + ([denominator] if divided else [])
+    shape = (count, share_rows, width)
     return pl.pallas_call(
-        functools.partial(collect_kernel, count, divided),
+        functools.partial(collect_kernel, count),
         out_shape=jax.ShapeDtypeStruct((share_rows, width), jnp.float32),
-        in_specs=[pl.BlockSpec(memory_space=pltpu.VMEM)] * len(operands),
+        in_specs=[pl.BlockSpec(memory_space=pltpu.VMEM)] * 2,
         out_specs=pl.BlockSpec(memory_space=pltpu.VMEM),
-        scratch_shapes=[
-            pltpu.VMEM((count, share_rows, width), jnp.float32),
-            pltpu.SemaphoreType.DMA((count,)),
-            pltpu.SemaphoreType.DMA((count,)),
-        ],
-        compiler_params=pltpu.CompilerParams(collective_id=number, has_side_effects=True),
-        name="collect" + str(number),
-    )(*operands)
+        scratch_shapes=[pltpu.VMEM(shape, jnp.float32)] * 2
+        + [pltpu.SemaphoreType.DMA((count,))] * 4,
+        compiler_params=pltpu.CompilerParams(collective_id=1, has_side_effects=True),
+        name="collect",
+    )(numerator.reshape(shape), denominator.reshape(shape))
 
 
 def local(row_count, col_count, row_data, row_baseline, pair_table, lengths, model_vis, gains):
@@ -420,7 +444,8 @@
     my_col = lax.axis_index("acol")
     first = pair_table[:, 0] - my_row * row_block
     second = pair_table[:, 1] - my_col * col_block
-    table = (lengths * row_block + first) * col_block + second
+    pair = first * (col_block // 2) + second // 2
+    table = ((pair << WEIGHT_BITS) + lengths) * (2 * col_block) + 2 * second
     table = jnp.concatenate([table, jnp.zeros((LANES,), jnp.int32)])
     outgoing, labels = route(row_data, row_baseline, devices, capacity, slots)
     names, column_gains = share(
@@ -438,9 +463,8 @@
         names.reshape(total), table, model_vis, column_gains.reshape(col_block, width)
     )
     power = segment(power_kernel, "power", info, [c], row_block, col_block)
-    denominator = collect(power, None, col_count, 1)
     product = segment(product_kernel, "product", info, [c, arrived], row_block, col_block)
-    return collect(product, denominator, col_count, 2)
+    return collect(product, power, col_count)
 
 
 def solution(mesh):

time: 120 us -> 101 us (0.84)
  Pallas kernels: 110 us -> 87.2 us
  waiting for transfers between devices: 0.01 us -> 4.07 us
    pallas_call x3 -> x2, Pallas kernels: 69 us -> 46.5 us  [the longest x1 35.7 us: gather(): pl.pallas_call(functools.partial(gather_kernel, col_block, chunk), out_sh...]
    all_to_all x1, waiting for transfers between devices: 0.01 us -> 4.07 us  [local(): lax.all_to_all(outgoing.reshape(devices, capacity, width), ('arow', 'acol...]
  transfers between devices with their start and end apart: 1 -> 1, of which waited for: 0 -> 1; matrix products, arithmetic and copies ran while one was open for 1% -> 1% of each run, Pallas kernels for 58% -> 44%
where the time goes in v2:
time: 101 us; the launch traced here: 100 us
  Pallas kernels  87.2 us (86%)
  starting transfers between devices  5.59 us (6%)
  waiting for transfers between devices  4.07 us (4%)
  local copies, waits for them, and re-layouts  3.31 us (3%)
    pallas_call x1, Pallas kernels, gather(): pl.pallas_call(functools.partial(gather_kernel, col_block, chunk), out_sh...  35.7 us
    pallas_call x2, Pallas kernels, segment(): pl.pallas_call(functools.partial(kernel, col_block), out_shape=jax.ShapeD...  17.5 us
    pallas_call x1, Pallas kernels, share(): pl.pallas_call(functools.partial(share_kernel, row_count, col_count), out...  12.5 us
    pallas_call x1, Pallas kernels, collect(): pl.pallas_call(functools.partial(collect_kernel, count), out_shape=jax.Sh...  10.8 us
    pallas_call x1, Pallas kernels, route(): pl.pallas_call(functools.partial(route_kernel, devices, capacity, slots),...  10.7 us
    all_to_all x1, starting transfers between devices, local(): lax.all_to_all(outgoing.reshape(devices, capacity, width), ('arow', 'acol...  5.59 us
    all_to_all x1, waiting for transfers between devices, local(): lax.all_to_all(outgoing.reshape(devices, capacity, width), ('arow', 'acol...  4.07 us
    unnamed x7, local copies, waits for them, and re-layouts  2.7 us
  transfers between devices with their start and end apart: 1, of which 1 were waited for; matrix products, arithmetic and copies ran while one was open for 1% of the time, Pallas kernels for 44%

profile of v2, /device:TPU:0, one launch (start us, length us, event | category | flops | bytes accessed | tf_op | source)
XLA Modules:
  0.0 100.3 jit_solution(2444633598304216073)
XLA Ops:
  0.0 0.0 copy-start.1
  0.0 0.0 copy-start.2
  0.0 10.7 %route.1 = (bf16[8192,128]{1,0:T(8,128)(2,1)}, s32[8192]{0:T(1024)}) custom-call(bf16[2048,128]{1,0:T(8,128)(2,1)} %rows_ref.1, s32[16,128]{1,0:T(8,128)} %bitcast.22), custom_call_target="tpu_custom_call" | custom-call | tf_op jit(solution)/shard_map/route/pallas_call | solution.py:77
  10.8 12.5 %share.1 = (s32[32,1,256]{2,1,0:T(1,128)}, f32[4,64,128]{2,1,0:T(8,128)}) custom-call(s32[32,1,256]{2,1,0:T(1,128)} %bitcast.21, f32[64,128]{1,0:T(8,128)} %gain_ref.1), custom_call_target="tpu_custom_call" | custom-call | tf_op jit(solution)/shard_map/share/pallas_call | solution.py:195
  23.3 5.6 %all-to-all-start = ((bf16[32,256,128]{2,1,0:T(8,128)(2,1)}), bf16[32,256,128]{2,1,0:T(8,128)(2,1)S(1)}, u32[]{:S(2)}, u32[]{:S(2)}) async-start(bf16[32,256,128]{2,1,0:T(8,128)(2,1)} %bitcast.13), calls=%async_computation | async-start | bytes 4194304 | tf_op jit(solution)/shard_map/all_to_all | solution.py:455
  28.9 0.0 copy-done.1
  28.9 0.0 copy-done.2
  29.0 0.6 concatenate.3.table_ref
  29.6 35.7 %gather.1 = (f32[8192,128]{1,0:T(8,128)}, s32[8192]{0:T(1024)}) custom-call(s32[8192]{0:T(1024)} %bitcast.20, s32[4224]{0:T(1024)} %concatenate.3.table_ref, bf16[65536,2,128]{2,1,0:T(2,128)(2,1)} %bitcast.12, f32[256,128]{1,0:T(8,128)} %bitcast.17), custom_call_target="tpu_custom_call" | custom-call | flops 1048576 | bytes 33554432 | tf_op jit(solution)/shard_map/gather/pallas_call | solution.py:275
  65.3 8.2 %power.1 = f32[512,128]{1,0:T(8,128)} custom-call(s32[8,1,1024]{2,1,0:T(1,128)} %bitcast.23, f32[8192,128]{1,0:T(8,128)} %get-tuple-element.19.c_ref), custom_call_target="tpu_custom_call" | custom-call | flops 2147483648 | bytes 4194304 | tf_op jit(solution)/shard_map/power/pallas_call | solution.py:361
  73.5 4.1 %all-to-all-done = bf16[32,256,128]{2,1,0:T(8,128)(2,1)S(1)} async-done(((bf16[32,256,128]{2,1,0:T(8,128)(2,1)}), bf16[32,256,128]{2,1,0:T(8,128)(2,1)S(1)}, u32[]{:S(2)}, u32[]{:S(2)}) %all-to-all-start) | async-done | bytes 2097184 | tf_op jit(solution)/shard_map/all_to_all | solution.py:455
  77.6 0.0 copy-start
  77.6 1.3 %copy-done = bf16[32,256,128]{2,1,0:T(8,128)(2,1)} copy-done((bf16[32,256,128]{2,1,0:T(8,128)(2,1)}, bf16[32,256,128]{2,1,0:T(8,128)(2,1)S(1)}, u32[]{:S(2)}) %copy-start) | copy-done | bytes 2097176
  78.9 9.2 %product.1 = f32[512,128]{1,0:T(8,128)} custom-call(s32[8,1,1024]{2,1,0:T(1,128)} %bitcast.24, f32[8192,128]{1,0:T(8,128)} %get-tuple-element.19.c_ref, bf16[8192,128]{1,0:T(8,128)(2,1)} %bitcast.14), custom_call_target="tpu_custom_call" | custom-call | flops 2147483648 | bytes 4194304 | tf_op jit(solution)/shard_map/product/pallas_call | solution.py:361
  88.2 10.8 %collect.1 = f32[64,128]{1,0:T(8,128)} custom-call(f32[8,64,128]{2,1,0:T(8,128)} %bitcast.16, f32[8,64,128]{2,1,0:T(8,128)} %bitcast.15), custom_call_target="tpu_custom_call" | custom-call | tf_op jit(solution)/shard_map/collect/pallas_call | solution.py:425
  98.9 1.4 %copy.8 = f32[64,128]{1,0:T(8,128)} copy(f32[64,128]{1,0:T(8,128)} %collect.1) | data formatting | bytes 65536
  (2 shorter events, 0.0 us)
Async XLA Ops:
  0.0 28.9 %copy-start.1 = (s32[4096,2]{0,1:T(2,128)S(1)}, s32[4096,2]{0,1:T(2,128)}, u32[]{:S(2)}) copy-start(s32[4096,2]{0,1:T(2,128)} %param.8) | copy-start | bytes 98308
  0.0 28.9 %copy-start.2 = (s32[4096]{0:T(1024)S(1)}, s32[4096]{0:T(1024)}, u32[]{:S(2)}) copy-start(s32[4096]{0:T(1024)} %param.9) | copy-start | bytes 49156
  23.3 54.3 %all-to-all-start = ((bf16[32,256,128]{2,1,0:T(8,128)(2,1)}), bf16[32,256,128]{2,1,0:T(8,128)(2,1)S(1)}, u32[]{:S(2)}, u32[]{:S(2)}) async-start(bf16[32,256,128]{2,1,0:T(8,128)(2,1)} %bitcast.13), calls=%async_computation | async-start | bytes 4194304 | tf_op jit(solution)/shard_map/all_to_all | solution.py:455
  77.6 1.3 %copy-start = (bf16[32,256,128]{2,1,0:T(8,128)(2,1)}, bf16[32,256,128]{2,1,0:T(8,128)(2,1)S(1)}, u32[]{:S(2)}) copy-start(bf16[32,256,128]{2,1,0:T(8,128)(2,1)S(1)} %all-to-all-done) | copy-start | bytes 6291460
